TPU v7x, 32 devices: a whole 2x2x4 slice. The times are simulated.
32 devices in a mesh: depth: 16 (over z, y, core), chan: 2 (over x).
Axes of the slice: x: 2, y: 2, z: 4, core: 2. Of those that a mesh axis runs over, the one named last changes fastest.
Arguments:
- pre: float32 [1, 512, 32, 256], P(None, 'chan', 'depth'), may hold values from -6 to 6
- grad_out: float32 [1, 512, 32, 256], P(None, 'chan', 'depth'), may hold values from -6 to 6
- weight: float32 [27, 512, 512], P(None, 'chan'), may hold values from -0.0546875 to 0.0546875
Outputs:
- grad_pre: float32 [1, 512, 32, 256], P(None, 'chan', 'depth')
- grad_weight: float32 [27, 512, 512], P(None, 'chan', 'depth')
All inputs are finite; a program needn't handle non-finite values.
Results may differ from a plain program's by a relative error of at most 0.0001.
Values sent between devices are 32-bit elements; how exact they have to be, the bound alone decides.
A program may use at most 192 MiB of HBM per device.

v0:
```python
import functools
import math

import jax
import jax.numpy as jnp
from jax import lax
from jax.experimental import pallas as pl
from jax.experimental.pallas import tpu as pltpu
from jax.sharding import PartitionSpec as P

W = 16
MESH = pl.DeviceIdType.MESH
F32, BF16 = jnp.float32, jnp.bfloat16


def normal_cdf(value):
    return 0.5 * (1.0 + lax.erf(value * (1.0 / math.sqrt(2.0))))


def split(value):
    high = value.astype(BF16)
    return high, (value - high.astype(F32)).astype(BF16)


def moved(value, drow, dcol):
    plane = value.shape[-1]
    lane = lax.broadcasted_iota(jnp.int32, value.shape, value.ndim - 1)
    step = drow * W + dcol
    turned = pltpu.roll(value, lax.rem(plane - step, plane), value.ndim - 1)
    col = lax.rem(lane, W) + dcol
    cell = lane + drow * W
    valid = (col >= 0) & (col < W) & (cell >= 0) & (cell < plane)
    return jnp.where(valid, turned, 0.0)


def dot(a, b):
    return jnp.dot(a, b, preferred_element_type=F32)


def dot_nt(a, b):
    return lax.dot_general(a, b, (((1,), (1,)), ((), ())), preferred_element_type=F32)


def kernel(far, near, scale, pre_ref, g_ref, w_ref, gp_ref, gw_ref,
           act, gs, fr, s_hi, s_lo, v_hi, v_lo, wb, acc, other, ga,
           local, gx_s, gx_r, h_s, h_r, hx_s, hx_r, a_r, a_s, f_s, f_r, t_s, t_r, e_s, e_r, w_sem):
    d, x = lax.axis_index("depth"), lax.axis_index("chan")
    nd, nc = lax.axis_size("depth"), lax.axis_size("chan")
    chips = far * near
    planes, cl, plane = pre_ref.shape
    ob = nc * cl // chips
    oc = ob // 2
    k, chip = lax.rem(d, 2), d // 2
    f, n = chip // near, lax.rem(chip, near)

    def dev(f_, n_, k_=None):
        return ((f_ * near + n_) * 2 + (k if k_ is None else k_), x)

    def remote(src, dst, ss, rs, to):
        return pltpu.make_async_remote_copy(src_ref=src, dst_ref=dst, send_sem=ss, recv_sem=rs, device_id=to, device_id_type=MESH)

    load_g = pltpu.make_async_copy(g_ref, gs.at[x, pl.ds(1, planes)], local.at[0])
    load_g.start()
    load_a = pltpu.make_async_copy(pre_ref, act.at[chip], local.at[1])
    load_a.start()

    bar = pltpu.get_barrier_semaphore()

    def hello(to):
        pl.semaphore_signal(bar, inc=1, device_id=to, device_id_type=MESH)

    for j in range(1, nc):
        hello((d, lax.rem(x + j, nc)))

    def hello_chip(j, carry):
        other_chip = lax.rem(chip + j, chips)
        hello((other_chip * 2 + k, x))
        return carry

    lax.fori_loop(1, chips, hello_chip, 0)
    hello((d + 1 - 2 * k, x))
    outer = d - 1 + 2 * k
    has_outer = (outer >= 0) & (outer < nd)

    @pl.when(has_outer)
    def _():
        hello((outer, x))

    pl.semaphore_wait(bar, nc - 1 + chips + jnp.where(has_outer, 1, 0))

    has = (d > 0, d < nd - 1)
    halo_in = []
    load_g.wait()
    to_next = remote(gs.at[x, planes], gs.at[x, 0], h_s.at[0], h_r.at[0], (d + 1, x))
    to_prev = remote(gs.at[x, 1], gs.at[x, planes + 1], h_s.at[1], h_r.at[1], (d - 1, x))

    @pl.when(has[1])
    def _():
        to_next.start()

    @pl.when(has[0])
    def _():
        to_prev.start()

    def g_send(j):
        to = (d, lax.rem(x + j, nc))
        span = pl.ds(1, planes)
        return remote(gs.at[x, span], gs.at[x, span], gx_s.at[j], gx_r.at[j], to)

    def halo_send(j, side):
        to = (d, lax.rem(x + j, nc))
        row = (0, planes + 1)[side]
        return remote(gs.at[x, row], gs.at[x, row], hx_s.at[j, side], hx_r.at[j, side], to)

    def g_recv(j):
        c = lax.rem(x + nc - j, nc)
        span = pl.ds(1, planes)
        return remote(gs.at[c, span], gs.at[c, span], gx_s.at[j], gx_r.at[j], (d, c))

    def halo_recv(j, side):
        c = lax.rem(x + nc - j, nc)
        row = (0, planes + 1)[side]
        return remote(gs.at[c, row], gs.at[c, row], hx_s.at[j, side], hx_r.at[j, side], (d, c))

    for j in range(1, nc):
        g_send(j).start()

    load_a.wait()

    def a_copy(slot, way, to):
        return remote(act.at[slot], act.at[slot], a_s.at[slot, way], a_r.at[slot], to)

    def a_forward(slot, up, down):
        @pl.when(up)
        def _():
            a_copy(slot, 0, dev(f + 1, n)).start()

        @pl.when(down)
        def _():
            a_copy(slot, 1, dev(f - 1, n)).start()

        for j in range(1, near):
            a_copy(slot, 1 + j, dev(f, lax.rem(n + j, near))).start()

    a_forward(chip, f < far - 1, f > 0)

    def relay(t):
        for sgn in range(2):
            f_ = f + (2 * sgn - 1) * t

            @pl.when((t < far) & (f_ >= 0) & (f_ < far))
            def _():
                slot = f_ * near + n
                a_copy(slot, 0, dev(f, n)).wait_recv()
                if sgn == 0:
                    a_forward(slot, f < far - 1, False)
                else:
                    a_forward(slot, False, f > 0)

    def f_copy(j):
        to_chip = lax.rem(chip + j, chips)
        first = to_chip * ob
        c, off = first // cl, pl.multiple_of(lax.rem(first, cl), ob)
        src = gs.at[c, pl.ds(1, planes), pl.ds(off, ob)]
        return c, remote(src, fr.at[chip, k], f_s.at[j], f_r.at[j], (to_chip * 2 + k, x))

    def f_start(mine):
        def step(j, carry):
            c, copy = f_copy(j)

            @pl.when((c == x) == mine)
            def _():
                copy.start()

            return carry

        lax.fori_loop(1, chips, step, 0)

    f_start(True)

    zero = jnp.zeros((cl, plane), F32)
    for side in range(2):
        @pl.when(jnp.logical_not(has[side]))
        def _():
            for c in range(nc):
                gs[c, (0, planes + 1)[side]] = zero

    ga[...] = jnp.zeros_like(ga)

    steps = nc * 9

    def chan_at(m):
        return lax.rem(x + nc - m, nc)

    def w_copy(step, kd):
        m, v = step // 9, lax.rem(step, 9)
        c, slot = chan_at(m), lax.rem(step, 2)
        src = w_ref.at[9 * kd + v, :, pl.ds(pl.multiple_of(c * cl, cl), cl)] if cl % 128 == 0 else w_ref.at[9 * kd + v]
        return pltpu.make_async_copy(src, wb.at[slot, kd], w_sem.at[slot, kd])

    for kd in range(3):
        w_copy(0, kd).start()

    def grad_act(m):
        c = chan_at(m)

        def body(v, carry):
            step = m * 9 + v
            slot = lax.rem(step, 2)

            @pl.when(step + 1 < steps)
            def _():
                for kd in range(3):
                    w_copy(step + 1, kd).start()

            drow, dcol = 1 - v // 3, 1 - lax.rem(v, 3)
            for q in range(planes + 2):
                hi, lo = split(moved(gs[c, q], drow, dcol))
                v_hi[:, pl.ds(q * plane, plane)] = hi
                v_lo[:, pl.ds(q * plane, plane)] = lo
            for kd in range(3):
                w_copy(step, kd).wait()
            total = None
            for kd in range(3):
                w = wb[slot, kd]
                if cl % 128 != 0:
                    pick = (lax.broadcasted_iota(jnp.int32, (w.shape[1], cl), 0)
                            == lax.broadcasted_iota(jnp.int32, (w.shape[1], cl), 1) + c * cl).astype(BF16)
                    w_hi, w_lo = split(w)
                    w_hi, w_lo = dot(w_hi, pick).astype(BF16), dot(w_lo, pick).astype(BF16)
                else:
                    w_hi, w_lo = split(w)
                span = pl.ds((2 - kd) * plane, planes * plane)
                part = dot(w_hi, v_hi[:, span]) + dot(w_lo, v_hi[:, span]) + dot(w_hi, v_lo[:, span])
                total = part if total is None else total + part
            ga[...] += total
            return carry

        lax.fori_loop(0, 9, body, 0)

    def halo_wait(side, copy):
        @pl.when(has[side])
        def _():
            copy()

    def own_halo(side):
        (to_next, to_prev)[side].wait_recv()
        for j in range(1, nc):
            halo_send(j, side).start()

    for side in range(2):
        halo_wait(side, functools.partial(own_halo, side))
    grad_act(0)
    relay(1)
    for j in range(1, nc):
        g_recv(j).wait_recv()
    f_start(False)
    first = chip * ob
    c0, off0 = first // cl, pl.multiple_of(lax.rem(first, cl), ob)
    mine = gs.at[c0, pl.ds(1, planes), pl.ds(off0, ob)]
    twin = (d + 1 - 2 * k, x)

    def t_copy(s, src):
        return remote(src, fr.at[s, k], t_s.at[s], t_r.at[s], twin)

    t_copy(chip, mine).start()
    for q in range(planes):
        fr[chip, k, q] = gs[c0, 1 + q, pl.ds(off0, ob)]
    for j in range(1, nc):
        for side in range(2):
            halo_wait(side, lambda: halo_recv(j, side).wait_recv())
        grad_act(j)
    own = act[chip]
    for q in range(planes):
        u = own[q]
        slope = normal_cdf(u) + u * jnp.exp(-0.5 * u * u) * (1.0 / math.sqrt(2.0 * math.pi))
        gp_ref[q] = ga[:, pl.ds(q * plane, plane)] * slope
    relay(2)

    def f_arrive(j, carry):
        s = lax.rem(chip + chips - j, chips)
        remote(fr.at[s, k], fr.at[s, k], f_s.at[j], f_r.at[j], (s * 2 + k, x)).wait_recv()
        t_copy(s, fr.at[s, k]).start()
        return carry

    lax.fori_loop(1, chips, f_arrive, 0)

    def t_arrive(s, carry):
        remote(fr.at[s, 1 - k], fr.at[s, 1 - k], t_s.at[s], t_r.at[s], twin).wait_recv()
        return carry

    lax.fori_loop(0, chips, t_arrive, 0)

    rows = 9 * oc
    for edge in (0, nd * planes + 1):
        s_hi[edge] = jnp.zeros(s_hi.shape[1:], BF16)
        s_lo[edge] = jnp.zeros(s_lo.shape[1:], BF16)

    def shifts(i, carry):
        s, c = i // 2, lax.rem(i, 2)
        for q in range(planes):
            block = fr[s, c, q]
            at = i * planes + q + 1
            for v in range(9):
                hi, lo = split(moved(block, 1 - v // 3, 1 - v % 3))
                for h in range(2):
                    s_hi[at, pl.ds(h * rows + v * oc, oc)] = hi[h * oc:(h + 1) * oc]
                    s_lo[at, pl.ds(h * rows + v * oc, oc)] = lo[h * oc:(h + 1) * oc]
        return carry

    lax.fori_loop(0, nd, shifts, 0)
    acc[...] = jnp.zeros_like(acc)

    def filter_block(s):
        parts = []
        for q in range(planes):
            u = act[s, q]
            parts.append(split(u * normal_cdf(u)))
        first_plane = (2 * s + k) * planes

        def body(kd, carry):
            total = None
            for q in range(planes):
                at = first_plane + q - kd + 2
                a_hi, a_lo = parts[q]
                part = dot_nt(s_hi[at], a_hi) + dot_nt(s_lo[at], a_hi) + dot_nt(s_hi[at], a_lo)
                total = part if total is None else total + part
            acc[kd] += total
            return carry

        for kd in range(3):
            body(kd, 0)

    def distance(t, carry):
        @pl.when(t >= 1)
        def _():
            relay(t + 2)

        def candidate(i, inner):
            j, sgn = i // 2, lax.rem(i, 2)
            dist = t - jnp.where(j > 0, 1, 0)
            f_ = f + (2 * sgn - 1) * dist
            valid = (dist >= 0) & (dist < far) & (f_ >= 0) & (f_ < far) & ((dist > 0) | (sgn == 0))

            @pl.when(valid)
            def _():
                slot = f_ * near + lax.rem(n + j, near)

                @pl.when(j > 0)
                def _():
                    a_copy(slot, 0, dev(f, n)).wait_recv()

                filter_block(slot)

            return inner

        lax.fori_loop(0, 2 * near, candidate, 0)
        return carry

    lax.fori_loop(0, far + 1, distance, 0)

    swap = remote(acc.at[:, pl.ds(pl.multiple_of((1 - k) * rows, rows), rows)], other, e_s.at[0], e_r.at[0], twin)
    swap.start()

    for j in range(1, nc):
        g_send(j).wait_send()
        for side in range(2):
            halo_wait(side, lambda: halo_send(j, side).wait_send())
    halo_wait(1, lambda: to_next.wait_send())
    halo_wait(0, lambda: to_prev.wait_send())

    def f_left(j, carry):
        f_copy(j)[1].wait_send()
        return carry

    lax.fori_loop(1, chips, f_left, 0)

    def t_left(s, carry):
        t_copy(s, fr.at[s, k]).wait_send()
        return carry

    lax.fori_loop(0, chips, t_left, 0)

    def a_left(f_, carry):
        slot = f_ * near + n

        @pl.when((f_ <= f) & (f < far - 1))
        def _():
            a_copy(slot, 0, dev(f + 1, n)).wait_send()

        @pl.when((f_ >= f) & (f > 0))
        def _():
            a_copy(slot, 1, dev(f - 1, n)).wait_send()

        for j in range(1, near):
            a_copy(slot, 1 + j, dev(f, lax.rem(n + j, near))).wait_send()
        return carry

    lax.fori_loop(0, far, a_left, 0)
    swap.wait()
    gw_ref[...] = (acc[:, pl.ds(pl.multiple_of(k * rows, rows), rows)] + other[...]) * scale


def shards(pre, grad_out, weight):
    batch, cl, planes, plane = pre.shape
    nd, nc = lax.axis_size("depth"), lax.axis_size("chan")
    chips = nd // 2
    far = math.gcd(chips, 4)
    near = chips // far
    outs = weight.shape[2]
    ob = outs // chips
    oc = ob // 2
    scale = float(batch * planes * nd * plane) ** (-0.5)
    cut = cl if cl % 128 == 0 else outs
    any_spec = pl.BlockSpec(memory_space=pl.ANY)
    vmem = pl.BlockSpec(memory_space=pltpu.VMEM)
    dma = pltpu.SemaphoreType.DMA
    rows = 9 * ob
    gp, gw = pl.pallas_call(
        functools.partial(kernel, far, near, scale),
        out_shape=(
            jax.ShapeDtypeStruct((planes, cl, plane), F32),
            jax.ShapeDtypeStruct((3, 9 * oc, cl), F32),
        ),
        in_specs=[any_spec, any_spec, any_spec],
        out_specs=(vmem, vmem),
        scratch_shapes=[
            pltpu.VMEM((chips, planes, cl, plane), F32),
            pltpu.VMEM((nc, planes + 2, cl, plane), F32),
            pltpu.VMEM((chips, 2, planes, ob, plane), F32),
            pltpu.VMEM((nd * planes + 2, rows, plane), BF16),
            pltpu.VMEM((nd * planes + 2, rows, plane), BF16),
            pltpu.VMEM((cl, (planes + 2) * plane), BF16),
            pltpu.VMEM((cl, (planes + 2) * plane), BF16),
            pltpu.VMEM((2, 3, cl, cut), F32),
            pltpu.VMEM((3, rows, cl), F32),
            pltpu.VMEM((3, 9 * oc, cl), F32),
            pltpu.VMEM((cl, planes * plane), F32),
            dma((2,)),
            dma((nc,)), dma((nc,)),
            dma((2,)), dma((2,)),
            dma((nc, 2)), dma((nc, 2)),
            dma((chips,)), dma((chips, 1 + near)),
            dma((chips,)), dma((chips,)),
            dma((chips,)), dma((chips,)),
            dma((1,)), dma((1,)),
            dma((2, 3)),
        ],
        compiler_params=pltpu.CompilerParams(
            collective_id=0, has_side_effects=True, vmem_limit_bytes=60 * 1024 * 1024
        ),
    )(pre[0].transpose(1, 0, 2), grad_out[0].transpose(1, 0, 2), weight)
    grad_pre = gp.transpose(1, 0, 2)[None]
    grad_weight = gw.reshape(27, oc, cl).transpose(0, 2, 1)
    return (grad_pre, grad_weight)


def solution(mesh):
    placed = (P(None, "chan", "depth", None), P(None, "chan", "depth", None), P(None, "chan", None))
    return jax.shard_map(
        shards,
        mesh=mesh,
        in_specs=placed,
        out_specs=(P(None, "chan", "depth", None), P(None, "chan", "depth")),
        check_vma=False,
    )
```

profile of v0, /device:TPU:21, one launch (start us, length us, event | category | flops | bytes accessed | tf_op | source)
XLA Modules:
  0.0 91.9 jit_solution(698502173758817208)
XLA Ops:
  0.6 2.3 %copy_bitcast_fusion = (f32[2,256,256]{2,1,0:T(8,128)}, f32[2,256,256]{2,1,0:T(8,128)}) fusion(f32[1,256,2,256]{3,2,1,0:T(2,128)} %param.4, f32[1,256,2,256]{3,2,1,0:T(2,128)} %param.3), kind=kLoop, calls=%fused_computation | loop fusion | bytes 2097152 | tf_op jit(solution)/shard_map/transpose | solution.py:452
  2.9 84.6 %shard_map.50 = (f32[2,256,256]{2,1,0:T(8,128)}, f32[3,288,256]{2,1,0:T(8,128)}) custom-call(f32[2,256,256]{2,1,0:T(8,128)} %get-tuple-element.9.pre_ref, f32[2,256,256]{2,1,0:T(8,128)} %get-tuple-element.8.g_ref, f32[27,256,512]{2,1,0:T(8,128)} %w_ref.1), custom_call_target="tpu_custom_call" | custom-call | tf_op jit(solution)/shard_map/pallas_call | solution.py:419
  87.5 2.2 %copy.7 = f32[1,256,2,256]{3,2,1,0:T(2,128)} copy(f32[1,256,2,256]{3,1,2,0:T(8,128)} %bitcast.15) | data formatting | bytes 1048576
  89.7 2.2 %copy.11 = f32[27,256,32]{1,2,0:T(8,128)} copy(f32[27,256,32]{1,2,0:T(8,128)} %bitcast.14) | data formatting | bytes 1769472
where the time goes:
time: 93.1 us; the launch traced here: 91.9 us
  Pallas kernels  84.6 us (91%)
  local copies, waits for them, and re-layouts  6.68 us (7%)
    pallas_call x1, Pallas kernels, shards(): pl.pallas_call(functools.partial(kernel, far, near, scale), out_shape=(ja...  84.6 us
    unnamed x2, local copies, waits for them, and re-layouts  4.41 us
    transpose x1, local copies, waits for them, and re-layouts, shards(): grad_out[0].transpose(1, 0, 2)  2.26 us

commit v1 on v0

--- a/solution.py
+++ b/solution.py
@@ -41,9 +41,9 @@
     return lax.dot_general(a, b, (((1,), (1,)), ((), ())), preferred_element_type=F32)
 
 
-def kernel(far, near, scale, pre_ref, g_ref, w_ref, gp_ref, gw_ref,
+def kernel(far, near, share, scale, pre_ref, g_ref, w_ref, gp_ref, gw_ref,
            act, gs, fr, s_hi, s_lo, v_hi, v_lo, wb, acc, other, ga,
-           local, gx_s, gx_r, h_s, h_r, hx_s, hx_r, a_r, a_s, f_s, f_r, t_s, t_r, e_s, e_r, w_sem):
+           local, gx_s, gx_r, h_s, h_r, hx_s, hx_r, a_r, a_s, f_s, f_r, fx_s, fx_r, t_s, t_r, e_s, e_r, w_sem):
     d, x = lax.axis_index("depth"), lax.axis_index("chan")
     nd, nc = lax.axis_size("depth"), lax.axis_size("chan")
     chips = far * near
@@ -59,6 +59,8 @@
     def remote(src, dst, ss, rs, to):
         return pltpu.make_async_remote_copy(src_ref=src, dst_ref=dst, send_sem=ss, recv_sem=rs, device_id=to, device_id_type=MESH)
 
+    twin = (d + 1 - 2 * k, x)
+
     load_g = pltpu.make_async_copy(g_ref, gs.at[x, pl.ds(1, planes)], local.at[0])
     load_g.start()
     load_a = pltpu.make_async_copy(pre_ref, act.at[chip], local.at[1])
@@ -89,7 +91,6 @@
     pl.semaphore_wait(bar, nc - 1 + chips + jnp.where(has_outer, 1, 0))
 
     has = (d > 0, d < nd - 1)
-    halo_in = []
     load_g.wait()
     to_next = remote(gs.at[x, planes], gs.at[x, 0], h_s.at[0], h_r.at[0], (d + 1, x))
     to_prev = remote(gs.at[x, 1], gs.at[x, planes + 1], h_s.at[1], h_r.at[1], (d - 1, x))
@@ -107,62 +108,96 @@
         span = pl.ds(1, planes)
         return remote(gs.at[x, span], gs.at[x, span], gx_s.at[j], gx_r.at[j], to)
 
-    def halo_send(j, side):
-        to = (d, lax.rem(x + j, nc))
-        row = (0, planes + 1)[side]
-        return remote(gs.at[x, row], gs.at[x, row], hx_s.at[j, side], hx_r.at[j, side], to)
+    def halo_outer(j, receive):
+        row = k * (planes + 1)
+        c = lax.rem(x + nc - j, nc) if receive else x
+        to = (d, c if receive else lax.rem(x + j, nc))
+        return remote(gs.at[c, row], gs.at[c, row], hx_s.at[j, 0], hx_r.at[j, 0], to)
+
+    def halo_inner(j, receive):
+        c = lax.rem(x + nc - j, nc)
+        dst = gs.at[c, (1 - k if receive else k) * (planes + 1)]
+        src = dst if receive else gs.at[c, planes - k * (planes - 1)]
+        return remote(src, dst, hx_s.at[j, 1], hx_r.at[j, 1], twin)
 
     def g_recv(j):
         c = lax.rem(x + nc - j, nc)
         span = pl.ds(1, planes)
         return remote(gs.at[c, span], gs.at[c, span], gx_s.at[j], gx_r.at[j], (d, c))
 
-    def halo_recv(j, side):
-        c = lax.rem(x + nc - j, nc)
-        row = (0, planes + 1)[side]
-        return remote(gs.at[c, row], gs.at[c, row], hx_s.at[j, side], hx_r.at[j, side], (d, c))
-
     for j in range(1, nc):
         g_send(j).start()
 
     load_a.wait()
 
-    def a_copy(slot, way, to):
-        return remote(act.at[slot], act.at[slot], a_s.at[slot, way], a_r.at[slot], to)
-
-    def a_forward(slot, up, down):
+    def a_copy(slot, q, way, to):
+        return remote(act.at[slot, q], act.at[slot, q], a_s.at[slot, q, way], a_r.at[slot, q], to)
+
+    last = planes - 1
+    low, high = f == 0, f == far - 1
+    low_next, high_next = (f == 1) & (far >= 4), (f == far - 2) & (far >= 4)
+
+    def column_sends(f_, q, run):
+        slot = f_ * near + n
+        ways = [
+            ((f_ <= f) & (f < far - 1), 0, dev(f + 1, n)),
+            ((f_ >= f) & (f > 0), 1, dev(f - 1, n)),
+        ]
+        around = (low_next & (f_ == 0)) | (high_next & (f_ == far - 1))
+        if q == last:
+            around = around | ((far >= 4) & ((low & (f_ == 1)) | (high & (f_ == far - 2))))
+        for j in range(1, near):
+            ways.append((jnp.logical_not(around), 1 + j, dev(f, lax.rem(n + j, near))))
+        for cond, way, to in ways:
+            @pl.when(cond)
+            def _():
+                run(a_copy(slot, q, way, to))
+
+    def layer_sends(j, q, run, late):
+        slot = f * near + lax.rem(n + j, near)
+        up, down = (high_next, low_next) if late else (low & (far >= 4), high & (far >= 4))
+
         @pl.when(up)
         def _():
-            a_copy(slot, 0, dev(f + 1, n)).start()
+            run(a_copy(slot, q, 0, dev(f + 1, n)))
 
         @pl.when(down)
         def _():
-            a_copy(slot, 1, dev(f - 1, n)).start()
-
-        for j in range(1, near):
-            a_copy(slot, 1 + j, dev(f, lax.rem(n + j, near))).start()
-
-    a_forward(chip, f < far - 1, f > 0)
-
-    def relay(t):
+            run(a_copy(slot, q, 1, dev(f - 1, n)))
+
+    def start(copy):
+        copy.start()
+
+    def left(copy):
+        copy.wait_send()
+
+    for q in range(planes):
+        column_sends(f, q, start)
+
+    def relay(t, q):
         for sgn in range(2):
             f_ = f + (2 * sgn - 1) * t
 
             @pl.when((t < far) & (f_ >= 0) & (f_ < far))
             def _():
-                slot = f_ * near + n
-                a_copy(slot, 0, dev(f, n)).wait_recv()
-                if sgn == 0:
-                    a_forward(slot, f < far - 1, False)
-                else:
-                    a_forward(slot, False, f > 0)
+                a_copy(f_ * near + n, q, 0, dev(f, n)).wait_recv()
+                column_sends(f_, q, start)
+
+    def relay_layer(q):
+        for j in range(1, near):
+            a_copy(f * near + lax.rem(n + j, near), q, 0, dev(f, n)).wait_recv()
+            layer_sends(j, q, start, False)
+
+    sub = ob // share
+    part, base = lax.rem(x, share), x - lax.rem(x, share)
 
     def f_copy(j):
         to_chip = lax.rem(chip + j, chips)
-        first = to_chip * ob
-        c, off = first // cl, pl.multiple_of(lax.rem(first, cl), ob)
-        src = gs.at[c, pl.ds(1, planes), pl.ds(off, ob)]
-        return c, remote(src, fr.at[chip, k], f_s.at[j], f_r.at[j], (to_chip * 2 + k, x))
+        at = to_chip * ob + part * sub
+        c, off = at // cl, pl.multiple_of(lax.rem(at, cl), sub)
+        src = gs.at[c, pl.ds(1, planes), pl.ds(off, sub)]
+        dst = fr.at[chip, k, :, pl.ds(pl.multiple_of(part * sub, sub), sub)]
+        return c, remote(src, dst, f_s.at[j], f_r.at[j], (to_chip * 2 + k, x))
 
     def f_start(mine):
         def step(j, carry):
@@ -201,7 +236,7 @@
     for kd in range(3):
         w_copy(0, kd).start()
 
-    def grad_act(m):
+    def grad_act(m, begin, end):
         c = chan_at(m)
 
         def body(v, carry):
@@ -236,29 +271,36 @@
             ga[...] += total
             return carry
 
-        lax.fori_loop(0, 9, body, 0)
+        lax.fori_loop(begin, end, body, 0)
 
     def halo_wait(side, copy):
         @pl.when(has[side])
         def _():
             copy()
 
-    def own_halo(side):
-        (to_next, to_prev)[side].wait_recv()
+    for side in range(2):
+        halo_wait(side, (to_next, to_prev)[side].wait_recv)
+
+    @pl.when(has_outer)
+    def _():
         for j in range(1, nc):
-            halo_send(j, side).start()
-
-    for side in range(2):
-        halo_wait(side, functools.partial(own_halo, side))
-    grad_act(0)
-    relay(1)
+            halo_outer(j, False).start()
+
+    grad_act(0, 0, 2)
+    relay_layer(0)
+    relay(1, 0)
+    grad_act(0, 2, 6)
+    for q in range(1, planes):
+        relay_layer(q)
+        relay(1, q)
     for j in range(1, nc):
         g_recv(j).wait_recv()
+        halo_inner(j, False).start()
     f_start(False)
+    grad_act(0, 6, 9)
     first = chip * ob
     c0, off0 = first // cl, pl.multiple_of(lax.rem(first, cl), ob)
     mine = gs.at[c0, pl.ds(1, planes), pl.ds(off0, ob)]
-    twin = (d + 1 - 2 * k, x)
 
     def t_copy(s, src):
         return remote(src, fr.at[s, k], t_s.at[s], t_r.at[s], twin)
@@ -267,23 +309,53 @@
     for q in range(planes):
         fr[chip, k, q] = gs[c0, 1 + q, pl.ds(off0, ob)]
     for j in range(1, nc):
-        for side in range(2):
-            halo_wait(side, lambda: halo_recv(j, side).wait_recv())
-        grad_act(j)
+        @pl.when(has_outer)
+        def _():
+            halo_outer(j, True).wait_recv()
+
+        halo_inner(j, True).wait_recv()
+    grad_act(1, 0, 3)
+    relay(2, 0)
+    grad_act(1, 3, 7)
+    for q in range(1, planes):
+        relay(2, q)
+    for j in range(1, near):
+        layer_sends(j, last, start, True)
+    grad_act(1, 7, 9)
+    for j in range(2, nc):
+        grad_act(j, 0, 9)
     own = act[chip]
     for q in range(planes):
         u = own[q]
         slope = normal_cdf(u) + u * jnp.exp(-0.5 * u * u) * (1.0 / math.sqrt(2.0 * math.pi))
         gp_ref[q] = ga[:, pl.ds(q * plane, plane)] * slope
-    relay(2)
+
+    def f_share(j, i):
+        src = fr.at[lax.rem(chip + chips - j, chips), k, :, pl.ds(pl.multiple_of(part * sub, sub), sub)]
+        return remote(src, src, fx_s.at[j, i], fx_r.at[j, i], (d, base + lax.rem(part + i, share)))
+
+    def f_shared(j, i):
+        theirs = lax.rem(part + share - i, share)
+        dst = fr.at[lax.rem(chip + chips - j, chips), k, :, pl.ds(pl.multiple_of(theirs * sub, sub), sub)]
+        return remote(dst, dst, fx_s.at[j, i], fx_r.at[j, i], (d, base + theirs))
 
     def f_arrive(j, carry):
+        src = fr.at[lax.rem(chip + chips - j, chips), k, :, pl.ds(pl.multiple_of(part * sub, sub), sub)]
+        remote(src, src, f_s.at[j], f_r.at[j], (d, x)).wait_recv()
+        for i in range(1, share):
+            f_share(j, i).start()
+        return carry
+
+    lax.fori_loop(1, chips, f_arrive, 0)
+
+    def x_arrive(j, carry):
+        for i in range(1, share):
+            f_shared(j, i).wait_recv()
         s = lax.rem(chip + chips - j, chips)
-        remote(fr.at[s, k], fr.at[s, k], f_s.at[j], f_r.at[j], (s * 2 + k, x)).wait_recv()
         t_copy(s, fr.at[s, k]).start()
         return carry
 
-    lax.fori_loop(1, chips, f_arrive, 0)
+    lax.fori_loop(1, chips, x_arrive, 0)
 
     def t_arrive(s, carry):
         remote(fr.at[s, 1 - k], fr.at[s, 1 - k], t_s.at[s], t_r.at[s], twin).wait_recv()
@@ -332,9 +404,10 @@
             body(kd, 0)
 
     def distance(t, carry):
-        @pl.when(t >= 1)
-        def _():
-            relay(t + 2)
+        @pl.when(t >= 2)
+        def _():
+            for q in range(planes):
+                relay(t + 2, q)
 
         def candidate(i, inner):
             j, sgn = i // 2, lax.rem(i, 2)
@@ -346,9 +419,10 @@
             def _():
                 slot = f_ * near + lax.rem(n + j, near)
 
-                @pl.when(j > 0)
+                @pl.when((j > 0) & (dist > 0))
                 def _():
-                    a_copy(slot, 0, dev(f, n)).wait_recv()
+                    for q in range(planes):
+                        a_copy(slot, q, 0, dev(f, n)).wait_recv()
 
                 filter_block(slot)
 
@@ -357,20 +431,30 @@
         lax.fori_loop(0, 2 * near, candidate, 0)
         return carry
 
-    lax.fori_loop(0, far + 1, distance, 0)
+    lax.fori_loop(0, 1, distance, 0)
+    relay(3, 0)
+    lax.fori_loop(1, 2, distance, 0)
+    for q in range(1, planes):
+        relay(3, q)
+    lax.fori_loop(2, far + 1, distance, 0)
 
     swap = remote(acc.at[:, pl.ds(pl.multiple_of((1 - k) * rows, rows), rows)], other, e_s.at[0], e_r.at[0], twin)
     swap.start()
 
     for j in range(1, nc):
         g_send(j).wait_send()
-        for side in range(2):
-            halo_wait(side, lambda: halo_send(j, side).wait_send())
+        halo_inner(j, False).wait_send()
+
+        @pl.when(has_outer)
+        def _():
+            halo_outer(j, False).wait_send()
     halo_wait(1, lambda: to_next.wait_send())
     halo_wait(0, lambda: to_prev.wait_send())
 
     def f_left(j, carry):
         f_copy(j)[1].wait_send()
+        for i in range(1, share):
+            f_share(j, i).wait_send()
         return carry
 
     lax.fori_loop(1, chips, f_left, 0)
@@ -382,21 +466,16 @@
     lax.fori_loop(0, chips, t_left, 0)
 
     def a_left(f_, carry):
-        slot = f_ * near + n
-
-        @pl.when((f_ <= f) & (f < far - 1))
-        def _():
-            a_copy(slot, 0, dev(f + 1, n)).wait_send()
-
-        @pl.when((f_ >= f) & (f > 0))
-        def _():
-            a_copy(slot, 1, dev(f - 1, n)).wait_send()
-
+        for q in range(planes):
+            column_sends(f_, q, left)
+        return carry
+
+    lax.fori_loop(0, far, a_left, 0)
+    for q in range(planes):
         for j in range(1, near):
-            a_copy(slot, 1 + j, dev(f, lax.rem(n + j, near))).wait_send()
-        return carry
-
-    lax.fori_loop(0, far, a_left, 0)
+            layer_sends(j, q, left, False)
+            if q == last:
+                layer_sends(j, q, left, True)
     swap.wait()
     gw_ref[...] = (acc[:, pl.ds(pl.multiple_of(k * rows, rows), rows)] + other[...]) * scale
 
@@ -410,6 +489,7 @@
     outs = weight.shape[2]
     ob = outs // chips
     oc = ob // 2
+    share = math.gcd(nc, max(ob // 8, 1))
     scale = float(batch * planes * nd * plane) ** (-0.5)
     cut = cl if cl % 128 == 0 else outs
     any_spec = pl.BlockSpec(memory_space=pl.ANY)
@@ -417,7 +497,7 @@
     dma = pltpu.SemaphoreType.DMA
     rows = 9 * ob
     gp, gw = pl.pallas_call(
-        functools.partial(kernel, far, near, scale),
+        functools.partial(kernel, far, near, share, scale),
         out_shape=(
             jax.ShapeDtypeStruct((planes, cl, plane), F32),
             jax.ShapeDtypeStruct((3, 9 * oc, cl), F32),
@@ -440,8 +520,9 @@
             dma((nc,)), dma((nc,)),
             dma((2,)), dma((2,)),
             dma((nc, 2)), dma((nc, 2)),
-            dma((chips,)), dma((chips, 1 + near)),
+            dma((chips, planes)), dma((chips, planes, 1 + near)),
             dma((chips,)), dma((chips,)),
+            dma((chips, share)), dma((chips, share)),
             dma((chips,)), dma((chips,)),
             dma((1,)), dma((1,)),
             dma((2, 3)),

time: 93.1 us -> 86.7 us (0.931); the launches traced: 91.9 us -> 86.5 us
  Pallas kernels: 84.6 us -> 79.2 us
    pallas_call x1, Pallas kernels: 84.6 us -> 79.2 us  [shards(): pl.pallas_call(functools.partial(kernel, far, near, share, scale), out_sh...]
where the time goes in v1:
time: 86.7 us; the launch traced here: 86.5 us
  Pallas kernels  79.2 us (91%)
  local copies, waits for them, and re-layouts  6.68 us (8%)
    pallas_call x1, Pallas kernels, shards(): pl.pallas_call(functools.partial(kernel, far, near, share, scale), out_sh...  79.2 us
    unnamed x2, local copies, waits for them, and re-layouts  4.41 us
    transpose x1, local copies, waits for them, and re-layouts, shards(): grad_out[0].transpose(1, 0, 2)  2.26 us

profile of v1, /device:TPU:21, one launch (start us, length us, event | category | flops | bytes accessed | tf_op | source)
XLA Modules:
  0.0 86.5 jit_solution(12620639521627956876)
XLA Ops:
  0.6 2.3 %copy_bitcast_fusion = (f32[2,256,256]{2,1,0:T(8,128)}, f32[2,256,256]{2,1,0:T(8,128)}) fusion(f32[1,256,2,256]{3,2,1,0:T(2,128)} %param.4, f32[1,256,2,256]{3,2,1,0:T(2,128)} %param.3), kind=kLoop, calls=%fused_computation | loop fusion | bytes 2097152 | tf_op jit(solution)/shard_map/transpose | solution.py:533
  2.9 79.2 %shard_map.50 = (f32[2,256,256]{2,1,0:T(8,128)}, f32[3,288,256]{2,1,0:T(8,128)}) custom-call(f32[2,256,256]{2,1,0:T(8,128)} %get-tuple-element.9.pre_ref, f32[2,256,256]{2,1,0:T(8,128)} %get-tuple-element.8.g_ref, f32[27,256,512]{2,1,0:T(8,128)} %w_ref.1), custom_call_target="tpu_custom_call" | custom-call | tf_op jit(solution)/shard_map/pallas_call | solution.py:499
  82.1 2.2 %copy.7 = f32[1,256,2,256]{3,2,1,0:T(2,128)} copy(f32[1,256,2,256]{3,1,2,0:T(8,128)} %bitcast.15) | data formatting | bytes 1048576
  84.3 2.2 %copy.11 = f32[27,256,32]{1,2,0:T(8,128)} copy(f32[27,256,32]{1,2,0:T(8,128)} %bitcast.14) | data formatting | bytes 1769472

commit v2 on v1

--- a/solution.py
+++ b/solution.py
@@ -127,6 +127,29 @@
 
     for j in range(1, nc):
         g_send(j).start()
+
+    sub = ob // share
+    part, base = lax.rem(x, share), x - lax.rem(x, share)
+
+    def f_copy(j):
+        to_chip = lax.rem(chip + j, chips)
+        at = to_chip * ob + part * sub
+        c, off = at // cl, pl.multiple_of(lax.rem(at, cl), sub)
+        src = gs.at[c, pl.ds(1, planes), pl.ds(off, sub)]
+        dst = fr.at[chip, k, :, pl.ds(pl.multiple_of(part * sub, sub), sub)]
+        return c, remote(src, dst, f_s.at[j], f_r.at[j], (to_chip * 2 + k, x))
+
+    def f_start(mine):
+        def step(j, carry):
+            c, copy = f_copy(j)
+
+            @pl.when((c == x) == mine)
+            def _():
+                copy.start()
+
+            return carry
+
+        lax.fori_loop(1, chips, step, 0)
 
     load_a.wait()
 
@@ -171,6 +194,7 @@
     def left(copy):
         copy.wait_send()
 
+    f_start(True)
     for q in range(planes):
         column_sends(f, q, start)
 
@@ -187,31 +211,6 @@
         for j in range(1, near):
             a_copy(f * near + lax.rem(n + j, near), q, 0, dev(f, n)).wait_recv()
             layer_sends(j, q, start, False)
-
-    sub = ob // share
-    part, base = lax.rem(x, share), x - lax.rem(x, share)
-
-    def f_copy(j):
-        to_chip = lax.rem(chip + j, chips)
-        at = to_chip * ob + part * sub
-        c, off = at // cl, pl.multiple_of(lax.rem(at, cl), sub)
-        src = gs.at[c, pl.ds(1, planes), pl.ds(off, sub)]
-        dst = fr.at[chip, k, :, pl.ds(pl.multiple_of(part * sub, sub), sub)]
-        return c, remote(src, dst, f_s.at[j], f_r.at[j], (to_chip * 2 + k, x))
-
-    def f_start(mine):
-        def step(j, carry):
-            c, copy = f_copy(j)
-
-            @pl.when((c == x) == mine)
-            def _():
-                copy.start()
-
-            return carry
-
-        lax.fori_loop(1, chips, step, 0)
-
-    f_start(True)
 
     zero = jnp.zeros((cl, plane), F32)
     for side in range(2):
@@ -290,13 +289,13 @@
     relay_layer(0)
     relay(1, 0)
     grad_act(0, 2, 6)
-    for q in range(1, planes):
-        relay_layer(q)
-        relay(1, q)
     for j in range(1, nc):
         g_recv(j).wait_recv()
         halo_inner(j, False).start()
     f_start(False)
+    for q in range(1, planes):
+        relay_layer(q)
+        relay(1, q)
     grad_act(0, 6, 9)
     first = chip * ob
     c0, off0 = first // cl, pl.multiple_of(lax.rem(first, cl), ob)
@@ -321,6 +320,33 @@
         relay(2, q)
     for j in range(1, near):
         layer_sends(j, last, start, True)
+    def f_share(j, i):
+        src = fr.at[lax.rem(chip + chips - j, chips), k, :, pl.ds(pl.multiple_of(part * sub, sub), sub)]
+        return remote(src, src, fx_s.at[j, i], fx_r.at[j, i], (d, base + lax.rem(part + i, share)))
+
+    def f_shared(j, i):
+        theirs = lax.rem(part + share - i, share)
+        dst = fr.at[lax.rem(chip + chips - j, chips), k, :, pl.ds(pl.multiple_of(theirs * sub, sub), sub)]
+        return remote(dst, dst, fx_s.at[j, i], fx_r.at[j, i], (d, base + theirs))
+
+    def f_arrive(j, carry):
+        src = fr.at[lax.rem(chip + chips - j, chips), k, :, pl.ds(pl.multiple_of(part * sub, sub), sub)]
+        remote(src, src, f_s.at[j], f_r.at[j], (d, x)).wait_recv()
+        for i in range(1, share):
+            f_share(j, i).start()
+        return carry
+
+    lax.fori_loop(1, chips, f_arrive, 0)
+
+    def x_arrive(j, carry):
+        for i in range(1, share):
+            f_shared(j, i).wait_recv()
+        s = lax.rem(chip + chips - j, chips)
+        t_copy(s, fr.at[s, k]).start()
+        return carry
+
+    lax.fori_loop(1, chips, x_arrive, 0)
+
     grad_act(1, 7, 9)
     for j in range(2, nc):
         grad_act(j, 0, 9)
@@ -329,33 +355,6 @@
         u = own[q]
         slope = normal_cdf(u) + u * jnp.exp(-0.5 * u * u) * (1.0 / math.sqrt(2.0 * math.pi))
         gp_ref[q] = ga[:, pl.ds(q * plane, plane)] * slope
-
-    def f_share(j, i):
-        src = fr.at[lax.rem(chip + chips - j, chips), k, :, pl.ds(pl.multiple_of(part * sub, sub), sub)]
-        return remote(src, src, fx_s.at[j, i], fx_r.at[j, i], (d, base + lax.rem(part + i, share)))
-
-    def f_shared(j, i):
-        theirs = lax.rem(part + share - i, share)
-        dst = fr.at[lax.rem(chip + chips - j, chips), k, :, pl.ds(pl.multiple_of(theirs * sub, sub), sub)]
-        return remote(dst, dst, fx_s.at[j, i], fx_r.at[j, i], (d, base + theirs))
-
-    def f_arrive(j, carry):
-        src = fr.at[lax.rem(chip + chips - j, chips), k, :, pl.ds(pl.multiple_of(part * sub, sub), sub)]
-        remote(src, src, f_s.at[j], f_r.at[j], (d, x)).wait_recv()
-        for i in range(1, share):
-            f_share(j, i).start()
-        return carry
-
-    lax.fori_loop(1, chips, f_arrive, 0)
-
-    def x_arrive(j, carry):
-        for i in range(1, share):
-            f_shared(j, i).wait_recv()
-        s = lax.rem(chip + chips - j, chips)
-        t_copy(s, fr.at[s, k]).start()
-        return carry
-
-    lax.fori_loop(1, chips, x_arrive, 0)
 
     def t_arrive(s, carry):
         remote(fr.at[s, 1 - k], fr.at[s, 1 - k], t_s.at[s], t_r.at[s], twin).wait_recv()

time: 86.7 us -> 94.5 us (1.090)
  the two profiles are of different devices: /device:TPU:21 before, /device:TPU:13 now
where the time goes in v2:
time: 94.5 us; the launch traced here: 94.2 us
  Pallas kernels  86.9 us (92%)
  local copies, waits for them, and re-layouts  6.68 us (7%)
    pallas_call x1, Pallas kernels, shards(): pl.pallas_call(functools.partial(kernel, far, near, share, scale), out_sh...  86.9 us
    unnamed x2, local copies, waits for them, and re-layouts  4.41 us
    transpose x1, local copies, waits for them, and re-layouts, shards(): grad_out[0].transpose(1, 0, 2)  2.26 us

profile of v2, /device:TPU:13, one launch (start us, length us, event | category | flops | bytes accessed | tf_op | source)
XLA Modules:
  0.0 94.2 jit_solution(5523421463932742488)
XLA Ops:
  0.6 2.3 %copy_bitcast_fusion = (f32[2,256,256]{2,1,0:T(8,128)}, f32[2,256,256]{2,1,0:T(8,128)}) fusion(f32[1,256,2,256]{3,2,1,0:T(2,128)} %param.4, f32[1,256,2,256]{3,2,1,0:T(2,128)} %param.3), kind=kLoop, calls=%fused_computation | loop fusion | bytes 2097152 | tf_op jit(solution)/shard_map/transpose | solution.py:532
  2.9 86.9 %shard_map.50 = (f32[2,256,256]{2,1,0:T(8,128)}, f32[3,288,256]{2,1,0:T(8,128)}) custom-call(f32[2,256,256]{2,1,0:T(8,128)} %get-tuple-element.9.pre_ref, f32[2,256,256]{2,1,0:T(8,128)} %get-tuple-element.8.g_ref, f32[27,256,512]{2,1,0:T(8,128)} %w_ref.1), custom_call_target="tpu_custom_call" | custom-call | tf_op jit(solution)/shard_map/pallas_call | solution.py:498
  89.8 2.2 %copy.7 = f32[1,256,2,256]{3,2,1,0:T(2,128)} copy(f32[1,256,2,256]{3,1,2,0:T(8,128)} %bitcast.15) | data formatting | bytes 1048576
  92.0 2.2 %copy.11 = f32[27,256,32]{1,2,0:T(8,128)} copy(f32[27,256,32]{1,2,0:T(8,128)} %bitcast.14) | data formatting | bytes 1769472
